TPU v7x, 16 devices: a 4x2x1 block of a 4x4x8 slice. The times are simulated.
16 devices in a mesh: rep: 4 (over y, z, core), pp: 4 (over x).
Axes of the slice: x: 4, y: 2, z: 1, core: 2. Of those that a mesh axis runs over, the one named last changes fastest.
The devices are a block of a 4x4x8 slice.
Arguments:
- x: bfloat16 [32, 512, 512], P('rep'), parts along dimension 0
- dy: bfloat16 [32, 512, 512], P('rep'), parts along dimension 0
- w_gate: bfloat16 [4, 512, 1408], P('pp')
- w_up: bfloat16 [4, 512, 1408], P('pp')
- w_down: bfloat16 [4, 1408, 512], P('pp')
Outputs:
- output 1: bfloat16 [16, 512, 1408], P(('rep', 'pp')), parts along dimension 0
- output 2: bfloat16 [16, 512, 1408], P(('rep', 'pp')), parts along dimension 0
- output 3: bfloat16 [16, 1408, 512], P(('rep', 'pp')), parts along dimension 0
There are 4 independent parts. A program takes and returns all parts, laid end to end along the dimension named above; an argument that names none is the same for every part.
All inputs are finite; a program needn't handle non-finite values.
Results may differ from a plain program's by a relative error of at most 0.018.
Values are sent between devices in bfloat16 or wider.
A program may use at most 768 MiB of HBM per device.

v0:
```python
import functools

import jax
import jax.numpy as jnp
from jax import lax
from jax.experimental import pallas as pl
from jax.experimental.pallas import tpu as pltpu
from jax.sharding import PartitionSpec as P

MESH = pl.DeviceIdType.MESH
F32, BF16 = jnp.float32, jnp.bfloat16
VMEM = 67_043_328
CHUNK = 128
LEAD = 8
OUT_SLOTS, BACK_SLOTS = 8, 8
EXTRA = 0


def dot(a, b):
    return jnp.dot(a, b, preferred_element_type=F32)


def dot_tokens(a, b):
    return lax.dot_general(a, b, (((0,), (0,)), ((), ())), preferred_element_type=F32)


def rounded(v):
    return v.astype(BF16).astype(F32)


def weight_work(ff):
    near = 1024
    return [
        [("d", 256 * i, 256) for i in range(near // 256)],
        [("d", near, ff - near)] + [("gu", 256 * j, 256) for j in range(0, 3)],
        [("gu", 256 * j, 256) for j in range(3, 7)],
        [("gu", 256 * j, 256) for j in range(7, 2 * ff // 256)],
    ]


def weight_terms(m, items, turn, tokens, dbuf, hid, dgu, abuf, abuf_t, accgu, accd, finish):
    two = pl.ds(pl.multiple_of(lax.rem(m, 2) * tokens, tokens), tokens)
    hid_at = pl.ds(pl.multiple_of(lax.rem(m, hid.shape[0] // tokens) * tokens, tokens), tokens)
    if turn:
        abuf_t[...] = abuf[two, :].T
    for kind, start, size in items:
        at = pl.ds(start, size)
        if kind == "gu":
            term = rounded(dot(abuf_t[...], dgu[two, at]))
            ref, where = accgu, (slice(None), at)
        else:
            term = rounded(dot_tokens(hid[hid_at, at], dbuf[pl.ds(pl.multiple_of(m * tokens, tokens), tokens), :]))
            ref, where = accd, (at, slice(None))
        if finish is None:
            ref[where] += term
        else:
            finish(kind, start, size, ref[where] + term)


def kernel(
    n, tokens, x_ref, dy_ref, wg_ref, wu_ref, wd_ref, dbuf, hid, dgu, abuf, accgu, accd,
    hbuf, hout, dout, pbuf, qbuf, abuf_t, wgu, wd, wgt, wut, wdt,
    w_sem, hrecv, drecv, hsend, dsend,
):
    total, dim = x_ref.shape
    ff = wd_ref.shape[1]
    per = tokens // CHUNK
    units = total // CHUNK
    slots = pbuf.shape[0]
    blocks = ff // 128
    me = lax.axis_index("pp")
    first, last = me == 0, me == n - 1
    lead = ((n - 1 - me) * LEAD) // 2 + jnp.where(first, EXTRA, 0)

    def rows_of(k):
        return pl.ds(pl.multiple_of(k * CHUNK, CHUNK), CHUNK)

    def ring(ref, k):
        return ref.at[pl.ds(pl.multiple_of(lax.rem(k, ref.shape[0] // CHUNK) * CHUNK, CHUNK), CHUNK)]

    def x_copy(k):
        rows = rows_of(k)
        return pltpu.make_async_copy(x_ref.at[rows], hbuf.at[rows], hrecv.at[k])

    def dy_copy(k):
        rows = rows_of(k)
        return pltpu.make_async_copy(dy_ref.at[rows], dbuf.at[rows], drecv.at[k])

    def h_copy(k):
        return pltpu.make_async_remote_copy(
            src_ref=hout.at[lax.rem(k, OUT_SLOTS)], dst_ref=hbuf.at[rows_of(k)],
            send_sem=hsend.at[k], recv_sem=hrecv.at[k], device_id={"pp": lax.rem(me + 1, n)}, device_id_type=MESH,
        )

    def d_copy(k):
        return pltpu.make_async_remote_copy(
            src_ref=dout.at[lax.rem(k, BACK_SLOTS)], dst_ref=dbuf.at[rows_of(k)],
            send_sem=dsend.at[k], recv_sem=drecv.at[k], device_id={"pp": lax.rem(me + n - 1, n)}, device_id_type=MESH,
        )

    loads = []
    for j in range(blocks):
        for i, ref in enumerate((wg_ref, wu_ref)):
            to = wgu.at[:, pl.ds(256 * j + 128 * i, 128)]
            loads.append(pltpu.make_async_copy(ref.at[0, :, pl.ds(128 * j, 128)], to, w_sem.at[2 * j + i]))
    loads.append(pltpu.make_async_copy(wd_ref.at[0], wd, w_sem.at[2 * blocks]))

    barrier = pltpu.get_barrier_semaphore()

    @pl.when(me > 0)
    def _():
        pl.semaphore_signal(barrier, inc=1, device_id={"pp": lax.rem(me + n - 1, n)}, device_id_type=MESH)

    @pl.when(me < n - 1)
    def _():
        pl.semaphore_signal(barrier, inc=1, device_id={"pp": lax.rem(me + 1, n)}, device_id_type=MESH)

    @pl.when(first)
    def _():
        x_copy(0).start()

    for load in loads:
        load.start()

    @pl.when(first)
    def _():
        @pl.loop(1, units)
        def _(k):
            x_copy(k).start()

    @pl.when(last)
    def _():
        @pl.loop(0, units)
        def _(k):
            dy_copy(k).start()

    for load in loads:
        load.wait()
    pl.semaphore_wait(barrier, jnp.where(first, 0, 1) + jnp.where(last, 0, 1))

    def prepare():
        for j in range(blocks):
            at = pl.ds(128 * j, 128)
            wgt[at, :] = wgu[:, pl.ds(256 * j, 128)].T
            wut[at, :] = wgu[:, pl.ds(256 * j + 128, 128)].T
            wdt[:, at] = wd[at, :].T
        accgu[...] = jnp.zeros_like(accgu)
        accd[...] = jnp.zeros_like(accd)

    def scaled(h):
        wide = h.astype(F32)
        scale = lax.rsqrt(jnp.mean(wide * wide, -1, keepdims=True) + 1e-6)
        return wide, scale, (wide * scale).astype(BF16)

    def hidden(k):
        slot, hid_part = lax.rem(k, slots), ring(hid, k)
        _, _, a = scaled(hbuf[rows_of(k), :])
        for j in range(blocks):
            both = dot(a, wgu[:, pl.ds(256 * j, 256)])
            gate, up = both[:, :128], both[:, 128:]
            s = jax.nn.sigmoid(gate)
            silu = gate * s
            at = pl.ds(128 * j, 128)
            pbuf[slot, :, at] = silu
            qbuf[slot, :, at] = up * (s + silu * (1.0 - s))
            hid_part[:, at] = (silu * up).astype(BF16)

    def forward(k, after):
        hidden(k)
        down = rounded(dot(ring(hid, k)[...], wd[...]))
        hout[lax.rem(k, OUT_SLOTS)] = (hbuf[rows_of(k), :].astype(F32) + down).astype(BF16)
        h_copy(k).start()
        after()

    def backward_hidden(k):
        slot, rows, dgu_part = lax.rem(k, slots), rows_of(k), ring(dgu, k)
        dy = dbuf[rows, :]
        wide, scale, a = scaled(hbuf[rows, :])
        ring(abuf, k)[...] = a
        for start in range(0, ff, 256):
            wide_by = min(256, ff - start)
            at = pl.ds(start, wide_by)
            dhid = rounded(dot(dy, wdt[:, at]))
            dgu_part[:, at] = (dhid * qbuf[slot, :, at]).astype(BF16)
            dgu_part[:, pl.ds(ff + start, wide_by)] = (dhid * pbuf[slot, :, at]).astype(BF16)
        return wide, scale

    def backward_input(k, wide, scale):
        dgu_part = ring(dgu, k)
        by_gate = rounded(dot(dgu_part[:, pl.ds(0, ff)], wgt[...]))
        by_up = rounded(dot(dgu_part[:, pl.ds(ff, ff)], wut[...]))
        da = rounded(by_gate + by_up)
        along = jnp.mean(da * wide, -1, keepdims=True)
        dn = rounded(da * scale - wide * (scale * scale * scale * along))
        dout[lax.rem(k, BACK_SLOTS)] = (dbuf[rows_of(k), :].astype(F32) + dn).astype(BF16)
        d_copy(k).start()

    def back_slot_free(k):
        @pl.when(k >= BACK_SLOTS)
        def _():
            d_copy(k - BACK_SLOTS).wait_send()

    def backward(k):
        backward_input(k, *backward_hidden(k))

    def forward_backward(k, after):
        hidden(k)
        backward_input(k, *backward_hidden(k))
        after()

    work = weight_work(ff)

    def weights(m, number):
        weight_terms(m, work[number], number == 0, tokens, dbuf, hid, dgu, abuf, abuf_t, accgu, accd, None)

    def with_weights(b, body):
        @pl.when(b < per)
        def _():
            body(lambda: None)

        for number in range(per):

            @pl.when((b >= per) & (lax.rem(b, per) == number))
            def _(number=number):
                body(lambda: weights(b // per - 1, number))

    @pl.loop(0, units + lead)
    def _(t):
        b = t - lead

        @pl.when(t == jnp.where(first, lead, 0))
        def _():
            prepare()

        @pl.when((t < units) & (me < n - 1))
        def _():
            @pl.when(first)
            def _():
                x_copy(t).wait()

            @pl.when(me > 0)
            def _():
                h_copy(t).wait_recv()

            @pl.when(t >= OUT_SLOTS)
            def _():
                h_copy(t - OUT_SLOTS).wait_send()

            with_weights(b, lambda after: forward(t, after))

        @pl.when(t >= units)
        def _():
            with_weights(b, lambda after: after())

        @pl.when((b >= 0) & first)
        def _():
            d_copy(b).wait_recv()
            backward_hidden(b)

        @pl.when((b >= 0) & (me > 0) & (me < n - 1))
        def _():
            d_copy(b).wait_recv()
            back_slot_free(b)
            backward(b)

        @pl.when(last)
        def _():
            dy_copy(b).wait()
            h_copy(b).wait_recv()
            back_slot_free(b)
            with_weights(b, lambda after: forward_backward(b, after))

    @pl.when(me < n - 1)
    def _():
        @pl.loop(units - OUT_SLOTS, units)
        def _(k):
            h_copy(k).wait_send()

    @pl.when(me > 0)
    def _():
        @pl.loop(units - BACK_SLOTS, units)
        def _(k):
            d_copy(k).wait_send()


def finish_kernel(micro, tokens, dbuf, hid, dgu, abuf, accgu, accd, og_ref, ou_ref, od_ref, gate_out, up_out, down_out, abuf_t, sem):
    ff, dim = accd.shape
    outs = []

    def finish(kind, start, size, value):
        value = value.astype(BF16)
        if kind == "d":
            down_out[pl.ds(start, size), :] = value
            return
        for ref, begin in ((gate_out, 0), (up_out, ff)):
            lo, hi = max(start, begin), min(start + size, begin + ff)
            if lo < hi:
                ref[:, pl.ds(lo - begin, hi - lo)] = value[:, lo - start : hi - start]

    def out(source, to):
        outs.append(pltpu.make_async_copy(source, to, sem.at[len(outs)]))
        outs[-1].start()

    done = {"d": 0, "gu": 0}
    for number, items in enumerate(weight_work(ff)):
        weight_terms(micro - 1, items, number == 0, tokens, dbuf, hid, dgu, abuf, abuf_t, accgu, accd, finish)
        begun = dict(done)
        for kind, start, size in items:
            done[kind] = start + size
        if done["d"] > begun["d"]:
            rows = pl.ds(begun["d"], done["d"] - begun["d"])
            out(down_out.at[rows], od_ref.at[0, rows])
        for buffer, to, begin in ((gate_out, og_ref, 0), (up_out, ou_ref, ff)):
            lo, hi = max(begun["gu"], begin), min(done["gu"], begin + ff)
            if lo < hi:
                columns = pl.ds(lo - begin, hi - lo)
                out(buffer.at[:, columns], to.at[0, :, columns])
    for copy in outs:
        copy.wait()


def solution(mesh):
    n = mesh.shape["pp"]

    def step(x, dy, w_gate, w_up, w_down):
        micro, tokens, dim = x.shape
        ff = w_down.shape[1]
        total = micro * tokens
        units = total // CHUNK
        slots = (n - 1) * LEAD // 2 + EXTRA + 1
        hid_rows = -(-(slots + 7) * CHUNK // tokens) * tokens
        any_space, in_vmem = pl.BlockSpec(memory_space=pl.ANY), pl.BlockSpec(memory_space=pltpu.VMEM)
        left = [
            pltpu.VMEM((total, dim), BF16),
            pltpu.VMEM((hid_rows, ff), BF16),
            pltpu.VMEM((2 * tokens, 2 * ff), BF16),
            pltpu.VMEM((2 * tokens, dim), BF16),
            pltpu.VMEM((dim, 2 * ff), F32),
            pltpu.VMEM((ff, dim), F32),
        ]
        scratch = [
            pltpu.VMEM((total, dim), BF16),
            pltpu.VMEM((OUT_SLOTS, CHUNK, dim), BF16),
            pltpu.VMEM((BACK_SLOTS, CHUNK, dim), BF16),
            pltpu.VMEM((slots, CHUNK, ff), F32),
            pltpu.VMEM((slots, CHUNK, ff), F32),
            pltpu.VMEM((dim, tokens), BF16),
            pltpu.VMEM((dim, 2 * ff), BF16),
            pltpu.VMEM((ff, dim), BF16),
            pltpu.VMEM((ff, dim), BF16),
            pltpu.VMEM((ff, dim), BF16),
            pltpu.VMEM((dim, ff), BF16),
            pltpu.SemaphoreType.DMA((2 * (ff // 128) + 1,)),
        ] + [pltpu.SemaphoreType.DMA((units,))] * 4
        left_bytes = 2 * (total * dim + hid_rows * ff + 2 * tokens * (2 * ff + dim)) + 4 * 3 * ff * dim
        state = pl.pallas_call(
            functools.partial(kernel, n, tokens),
            out_shape=left,
            in_specs=[any_space] * 5,
            out_specs=[in_vmem] * len(left),
            scratch_shapes=scratch,
            compiler_params=pltpu.CompilerParams(
                collective_id=0, has_side_effects=True, vmem_limit_bytes=VMEM - left_bytes - (64 << 10)
            ),
        )(x.reshape(total, dim), dy.reshape(total, dim), w_gate, w_up, w_down)
        return pl.pallas_call(
            functools.partial(finish_kernel, micro, tokens),
            out_shape=[jax.ShapeDtypeStruct(w.shape, BF16) for w in (w_gate, w_up, w_down)],
            in_specs=[in_vmem] * len(left),
            out_specs=[any_space] * 3,
            scratch_shapes=[
                pltpu.VMEM((dim, ff), BF16),
                pltpu.VMEM((dim, ff), BF16),
                pltpu.VMEM((ff, dim), BF16),
                pltpu.VMEM((dim, tokens), BF16),
                pltpu.SemaphoreType.DMA((8,)),
            ],
            compiler_params=pltpu.CompilerParams(vmem_limit_bytes=8 << 20),
        )(*state)

    return jax.shard_map(
        step,
        mesh=mesh,
        in_specs=(P("rep", None, None),) * 2 + (P("pp", None, None),) * 3,
        out_specs=(P(("rep", "pp"), None, None),) * 3,
        check_vma=False,
    )
```

profile of v0, /device:TPU:112, one launch (start us, length us, event | category | flops | bytes accessed | tf_op | source)
XLA Modules:
  0.0 131.5 jit_solution(7307324623671826732)
XLA Ops:
  0.6 127.2 %shard_map.76 = (bf16[4096,512]{1,0:T(8,128)(2,1)S(1)}, bf16[2560,1408]{1,0:T(8,128)(2,1)S(1)}, bf16[1024,2816]{1,0:T(8,128)(2,1)S(1)}, bf16[1024,512]{1,0:T(8,1...) custom-call(bf16[4096,512]{1,0:T(8,128)(2,1)} %bitcast.2, bf16[4096,512]{1,0:T(8,128)(2,1)} %bitcast.3, ...), custom_call_target="tpu_custom_call" | custom-call | tf_op jit(solution)/shard_map/pallas_call | solution.py:356
  127.8 3.5 %shard_map.77 = (bf16[1,512,1408]{2,1,0:T(8,128)(2,1)}, bf16[1,512,1408]{2,1,0:T(8,128)(2,1)}, bf16[1,1408,512]{2,1,0:T(8,128)(2,1)}) custom-call(bf16[4096,512]{1,0:T(8,128)(2,1)S(1)} %get-tuple-element.9.dbuf, bf16[2560,1408]{1,0:T(8,128)(2,1)S(1)} %get-tuple-element.10.hid, bf16[1024,2816]{1,0:T(8,128)(2,1)S(1)} %get-tuple-element.11.dgu, ...), custom_call_target="tpu_custom_call" | custom-call | tf_op jit(solution)/shard_map/pallas_call | solution.py:366
where the time goes:
time: 132 us; the launch traced here: 131 us
  Pallas kernels  131 us (99%)
    pallas_call x1, Pallas kernels, step(): pl.pallas_call(functools.partial(kernel, n, tokens), out_shape=left, in_s...  127 us
    pallas_call x1, Pallas kernels, step(): pl.pallas_call(functools.partial(finish_kernel, micro, tokens), out_shape...  3.49 us

commit v1 on v0

--- a/solution.py
+++ b/solution.py
@@ -59,7 +59,7 @@
 
 def kernel(
     n, tokens, x_ref, dy_ref, wg_ref, wu_ref, wd_ref, dbuf, hid, dgu, abuf, accgu, accd,
-    hbuf, hout, dout, pbuf, qbuf, abuf_t, wgu, wd, wgt, wut, wdt,
+    hbuf, hout, dout, pbuf, qbuf, dhid_buf, abuf_t, wgu, wd, wgt, wut, wdt,
     w_sem, hrecv, drecv, hsend, dsend,
 ):
     total, dim = x_ref.shape
@@ -134,8 +134,13 @@
         def _(k):
             dy_copy(k).start()
 
-    for load in loads:
+    for load in loads[:-1]:
         load.wait()
+
+    @pl.when(me > 0)
+    def _():
+        loads[-1].wait()
+
     pl.semaphore_wait(barrier, jnp.where(first, 0, 1) + jnp.where(last, 0, 1))
 
     def prepare():
@@ -165,14 +170,16 @@
             qbuf[slot, :, at] = up * (s + silu * (1.0 - s))
             hid_part[:, at] = (silu * up).astype(BF16)
 
-    def forward(k, after):
+    def forward(k, after, load=None):
         hidden(k)
+        if load:
+            load.wait()
         down = rounded(dot(ring(hid, k)[...], wd[...]))
         hout[lax.rem(k, OUT_SLOTS)] = (hbuf[rows_of(k), :].astype(F32) + down).astype(BF16)
         h_copy(k).start()
         after()
 
-    def backward_hidden(k):
+    def backward_hidden(k, ready=False):
         slot, rows, dgu_part = lax.rem(k, slots), rows_of(k), ring(dgu, k)
         dy = dbuf[rows, :]
         wide, scale, a = scaled(hbuf[rows, :])
@@ -180,7 +187,7 @@
         for start in range(0, ff, 256):
             wide_by = min(256, ff - start)
             at = pl.ds(start, wide_by)
-            dhid = rounded(dot(dy, wdt[:, at]))
+            dhid = dhid_buf[:, at].astype(F32) if ready else rounded(dot(dy, wdt[:, at]))
             dgu_part[:, at] = (dhid * qbuf[slot, :, at]).astype(BF16)
             dgu_part[:, pl.ds(ff + start, wide_by)] = (dhid * pbuf[slot, :, at]).astype(BF16)
         return wide, scale
@@ -205,7 +212,7 @@
 
     def forward_backward(k, after):
         hidden(k)
-        backward_input(k, *backward_hidden(k))
+        backward_input(k, *backward_hidden(k, ready=True))
         after()
 
     work = weight_work(ff)
@@ -246,7 +253,13 @@
             def _():
                 h_copy(t - OUT_SLOTS).wait_send()
 
-            with_weights(b, lambda after: forward(t, after))
+            @pl.when(first & (t == 0))
+            def _():
+                forward(t, lambda: None, loads[-1])
+
+            @pl.when((me > 0) | (t > 0))
+            def _():
+                with_weights(b, lambda after: forward(t, after))
 
         @pl.when(t >= units)
         def _():
@@ -266,8 +279,9 @@
         @pl.when(last)
         def _():
             dy_copy(b).wait()
+            back_slot_free(b)
+            dhid_buf[...] = dot(dbuf[rows_of(b), :], wdt[...]).astype(BF16)
             h_copy(b).wait_recv()
-            back_slot_free(b)
             with_weights(b, lambda after: forward_backward(b, after))
 
     @pl.when(me < n - 1)
@@ -302,7 +316,10 @@
         outs[-1].start()
 
     done = {"d": 0, "gu": 0}
-    for number, items in enumerate(weight_work(ff)):
+    near, *rest = weight_work(ff)
+    wide = [item for part in rest for item in part if item[0] == "gu"]
+    narrow = [item for part in rest for item in part if item[0] == "d"]
+    for number, items in enumerate([near, wide[:4], wide[4:8], wide[8:], narrow]):
         weight_terms(micro - 1, items, number == 0, tokens, dbuf, hid, dgu, abuf, abuf_t, accgu, accd, finish)
         begun = dict(done)
         for kind, start, size in items:
@@ -344,6 +361,7 @@
             pltpu.VMEM((BACK_SLOTS, CHUNK, dim), BF16),
             pltpu.VMEM((slots, CHUNK, ff), F32),
             pltpu.VMEM((slots, CHUNK, ff), F32),
+            pltpu.VMEM((CHUNK, ff), BF16),
             pltpu.VMEM((dim, tokens), BF16),
             pltpu.VMEM((dim, 2 * ff), BF16),
             pltpu.VMEM((ff, dim), BF16),

time: 132 us -> 132 us (level)
  no operation moved by 1% of the time
where the time goes in v1:
time: 132 us
  Pallas kernels  131 us (99%)
    pallas_call x1, Pallas kernels, step(): pl.pallas_call(functools.partial(kernel, n, tokens), out_shape=left, in_s...  127 us
    pallas_call x1, Pallas kernels, step(): pl.pallas_call(functools.partial(finish_kernel, micro, tokens), out_shape...  3.54 us

profile of v1, /device:TPU:112, one launch (start us, length us, event | category | flops | bytes accessed | tf_op | source)
XLA Modules:
  0.0 131.6 jit_solution(8278006642495207770)
XLA Ops:
  0.6 127.3 %shard_map.76 = (bf16[4096,512]{1,0:T(8,128)(2,1)S(1)}, bf16[2560,1408]{1,0:T(8,128)(2,1)S(1)}, bf16[1024,2816]{1,0:T(8,128)(2,1)S(1)}, bf16[1024,512]{1,0:T(8,1...) custom-call(bf16[4096,512]{1,0:T(8,128)(2,1)} %bitcast.2, bf16[4096,512]{1,0:T(8,128)(2,1)} %bitcast.3, ...), custom_call_target="tpu_custom_call" | custom-call | tf_op jit(solution)/shard_map/pallas_call | solution.py:374
  127.9 3.5 %shard_map.77 = (bf16[1,512,1408]{2,1,0:T(8,128)(2,1)}, bf16[1,512,1408]{2,1,0:T(8,128)(2,1)}, bf16[1,1408,512]{2,1,0:T(8,128)(2,1)}) custom-call(bf16[4096,512]{1,0:T(8,128)(2,1)S(1)} %get-tuple-element.9.dbuf, bf16[2560,1408]{1,0:T(8,128)(2,1)S(1)} %get-tuple-element.10.hid, bf16[1024,2816]{1,0:T(8,128)(2,1)S(1)} %get-tuple-element.11.dgu, ...), custom_call_target="tpu_custom_call" | custom-call | tf_op jit(solution)/shard_map/pallas_call | solution.py:384
